TPU v7x, 32 devices: a whole 2x2x4 slice. The times are simulated.
32 devices in a mesh: row: 4 (over z), col: 8 (over y, x, core).
Axes of the slice: x: 2, y: 2, z: 4, core: 2. Of those that a mesh axis runs over, the one named last changes fastest.
Arguments:
- matrix: float32 [32, 512, 16, 1024], P(None, 'row', None, 'col'), may hold values from -150 to 150
- inverse_rest: float32 [32, 512, 14, 1024], P(None, 'row', None, 'col'), may hold values from -6 to 6
- upper_block: float32 [4, 512, 2, 1024], P(None, 'row', None, 'col'), may hold values from -6 to 6, as said below
- lower_below: float32 [4, 512, 14, 1024], P(None, 'row', None, 'col'), may hold values from -0.046875 to 0.046875
- lower_inverse: float32 [4, 512, 2048], P(None, 'row', 'col'), may hold values from -1 to 1, as said below
Outputs:
- plus_rows: float32 [4, 512, 16, 1024], P(None, 'row', None, 'col')
Inputs may be any that keep to these rules, and one draw needn't show every extreme that they name: `upper_block`: upper triangular. `lower_inverse`: unit lower triangular.
All inputs are finite; a program needn't handle non-finite values.
Results may differ from a plain program's by a relative error of at most 0.000052.
Values sent between devices are 32-bit elements; how exact they have to be, the bound alone decides.
A program may use at most 256 MiB of HBM per device.

v0:
```python
import functools

import jax
import jax.numpy as jnp
from jax import lax
from jax.experimental import pallas as pl
from jax.experimental.pallas import tpu as pltpu
from jax.sharding import PartitionSpec as P

MESH = pl.DeviceIdType.MESH


def halvings(col_devices):
    bits = col_devices.bit_length() - 1
    return [[0] + list(range(1, bits)), [0] + list(range(bits - 1, 0, -1))]


def held(order, stage, col_devices):
    cleared = sum(1 << b for b in order[: stage + 1])
    return [m for m in range(col_devices) if m & cleared == 0]


def panel_kernel(
    rows_n, cols_n, steps_of,
    matrix_ref, rest_ref, below_ref, upper_ref, lower_ref, mirror_ref, factor_ref, total_ref,
    land, raw, left, right, sums, update, pair, tile, total, outbox, squares, panes, stats, *more,
):
    stages = cols_n.bit_length() - 1
    recvs, more = more[:stages], more[stages:]
    (own_sem, raw_sem, zsend, zrecv, csend, crecv, cfree, hsend, hrecv, hfree) = more[:10]
    (lower_sem, fzsend, fzrecv, fsend, frecv, tile_sem, msend, mrecv, pane_sem, ssem, rsem) = more[10:]
    _, _, _, wide, _ = factor_ref.shape
    span = tile.shape[1]
    outer = mirror_ref.shape[2]
    ratio = cols_n // rows_n
    cycles, _, groups, blk, lanes_n = land.shape
    depth = groups * lanes_n
    share = right.shape[0]
    half_rows = sums.shape[2]
    blocks, part = raw.shape[1], raw.shape[3]
    half = cols_n // 2
    orders = halvings(cols_n)
    z, c = lax.axis_index("row"), lax.axis_index("col")

    def peer(bit):
        return lax.bitwise_xor(c, jnp.int32(1 << bit))

    def cyc_of(it):
        return cycles - 1 - it

    barrier = pltpu.get_barrier_semaphore()
    me = z * cols_n + c
    everyone = rows_n * cols_n

    def greet(step, _):
        other = lax.rem(me + step, everyone)
        pl.semaphore_signal(
            barrier, inc=1, device_id=(other // cols_n, lax.rem(other, cols_n)), device_id_type=MESH
        )
        return 0

    lax.fori_loop(1, everyone, greet, 0)
    own = pltpu.make_async_copy(below_ref, land.at[:, z], own_sem)
    own.start()
    lower = pltpu.make_async_copy(lower_ref, factor_ref.at[:, z, c], lower_sem)
    lower.start()

    def m_of(k):
        return jnp.where(k < half, cols_n - 1 - 2 * k, 2 * (cols_n - 1 - k))

    def raw_copy(k, slot):
        s = lax.bitwise_xor(m_of(k), c)
        group = s * part // blk * blocks
        begin = pl.multiple_of(lax.rem(s * part, blk), part)
        return pltpu.make_async_copy(
            rest_ref.at[pl.ds(group, blocks), :, pl.ds(begin, part)], raw.at[slot], raw_sem.at[slot]
        )

    raw_copy(0, 0).start()
    own.wait()
    lower.wait()
    pl.semaphore_wait(barrier, everyone - 1)

    def piece(kind, cyc, source, to, way):
        block = factor_ref.at[cyc, source, c] if kind else land.at[cyc, source]
        return pltpu.make_async_remote_copy(
            src_ref=block,
            dst_ref=block,
            send_sem=(fzsend if kind else zsend).at[cyc, source, way],
            recv_sem=(fzrecv if kind else zrecv).at[cyc, source],
            device_id=(to, c),
            device_id_type=MESH,
        )

    def send_own(cyc):
        for kind in range(2):
            @pl.when(z < rows_n - 1)
            def _():
                piece(kind, cyc, z, z + 1, 0).start()

            @pl.when(z > 0)
            def _():
                piece(kind, cyc, z, z - 1, 1).start()

    inner = (z > 0) & (z < rows_n - 1)

    def arrive(cyc, forward):
        for t in range(1, rows_n):
            for kind in range(2):
                @pl.when((z >= t) & (inner == forward))
                def _():
                    piece(kind, cyc, z - t, z, 0).wait_recv()
                    if forward:
                        piece(kind, cyc, z - t, z + 1, 0).start()

                @pl.when((z + t < rows_n) & (inner == forward))
                def _():
                    piece(kind, cyc, z + t, z, 0).wait_recv()
                    if forward:
                        piece(kind, cyc, z + t, z - 1, 1).start()

    def relay(cyc):
        arrive(cyc, True)

        @pl.when(inner & (cyc > 0))
        def _():
            send_own(cyc - 1)

    @pl.when(inner)
    def _():
        send_own(cycles - 1)

    @pl.when(jnp.logical_not(inner))
    def _():
        for at in range(cycles):
            send_own(cycles - 1 - at)

    relay(cycles - 1)

    def pane_copy(at, slot):
        return pltpu.make_async_copy(matrix_ref.at[at], panes.at[slot], pane_sem.at[slot])

    pane_copy(0, 0).start()
    squares[...] = jnp.zeros_like(squares)

    def pane_step(at, _):
        slot = lax.rem(at, 2)
        pane_copy(at, slot).wait()

        @pl.when(at + 1 < matrix_ref.shape[0])
        def _():
            pane_copy(at + 1, 1 - slot).start()

        value = panes[slot].reshape(-1, 8, lanes_n)
        squares[0] += jnp.sum(value * value, axis=0)
        return 0

    lax.fori_loop(0, matrix_ref.shape[0], pane_step, 0)

    def spread(cyc, source, to, at):
        return pltpu.make_async_remote_copy(
            src_ref=factor_ref.at[cyc, :, source],
            dst_ref=factor_ref.at[cyc, :, source],
            send_sem=fsend.at[cyc, at],
            recv_sem=frecv.at[cyc, at],
            device_id=(z, to),
            device_id_type=MESH,
        )

    def factor_start(cyc):
        for e in [1] + list(range(2, cols_n, 2)):
            spread(cyc, c, lax.bitwise_xor(c, jnp.int32(e)), e).start()

    def factor_pass(cyc):
        for e in range(2, cols_n, 2):
            other = lax.bitwise_xor(c, jnp.int32(e))
            spread(cyc, other, other, e).wait_recv()
            spread(cyc, other, peer(0), e ^ 1).start()

    def factor_wait(cyc):
        for e in range(1, cols_n, 2):
            other = lax.bitwise_xor(c, jnp.int32(e))
            spread(cyc, other, other, e).wait_recv()

    def away(cyc, to, turn):
        return pltpu.make_async_remote_copy(
            src_ref=outbox.at[to, turn],
            dst_ref=mirror_ref.at[cyc, c],
            send_sem=msend.at[to, turn],
            recv_sem=mrecv.at[cyc, c],
            device_id=(to, turn * rows_n + z),
            device_id_type=MESH,
        )

    def at_home(cyc, to, turn):
        return pltpu.make_async_copy(
            outbox.at[to, turn], mirror_ref.at[cyc, c], msend.at[to, turn]
        )

    def is_home(to, turn):
        return (z == to) & (turn * rows_n + z == c)

    def mail_wait(cyc):
        for to in range(rows_n):
            for turn in range(ratio):
                @pl.when(is_home(to, turn))
                def _():
                    at_home(cyc, to, turn).wait()

                @pl.when(jnp.logical_not(is_home(to, turn)))
                def _():
                    away(cyc, to, turn).wait_send()

    def panel_step(it):
        cyc = cyc_of(it)
        factor_wait(cyc)

        def tile_step(back, _):
            from_cyc = cycles - 1 - back
            copy = pltpu.make_async_copy(
                factor_ref.at[from_cyc, :, pl.ds(cyc * span, span)], tile, tile_sem
            )
            copy.start()
            copy.wait()
            for source in range(rows_n):
                for column in range(span):
                    value = tile[source, column]
                    high = value.astype(jnp.bfloat16)
                    low = (value - high.astype(jnp.float32)).astype(jnp.bfloat16)
                    rows = slice(column * wide, (column + 1) * wide)
                    cols = slice(source * blk, (source + 1) * blk)
                    pair[0, rows, cols] = high
                    pair[1, rows, cols] = low
            product = None
            for one, two in ((0, 0), (0, 1), (1, 0)):
                term = jnp.dot(pair[one], update[from_cyc, two], preferred_element_type=jnp.float32)
                product = term if product is None else product + term

            @pl.when(back == 0)
            def _():
                total[...] = product

            @pl.when(back > 0)
            def _():
                total[...] += product

            return 0

        lax.fori_loop(0, it + 1, tile_step, 0)

        @pl.when(it > 0)
        def _():
            mail_wait(cyc + 1)

        for to in range(rows_n):
            value = total[to * blk : (to + 1) * blk, :]
            square = value * value
            partial = jnp.sum(square.reshape(blk // 8, 8, share), axis=0)
            for lane in range(0, share, lanes_n):
                squares[1] += partial[:, lane : lane + lanes_n]
            for turn in range(ratio):
                for place in range(outer):
                    begin = (place * ratio + turn) * part
                    outbox[to, turn, place] = value[:, begin : begin + part]
        for to in range(rows_n):
            for turn in range(ratio):
                @pl.when(is_home(to, turn))
                def _():
                    at_home(cyc, to, turn).start()

                @pl.when(jnp.logical_not(is_home(to, turn)))
                def _():
                    away(cyc, to, turn).start()

    def core_copy(m):
        slot = m // 2
        return pltpu.make_async_remote_copy(
            src_ref=sums.at[:, m],
            dst_ref=recvs[0].at[:, slot],
            send_sem=csend.at[slot],
            recv_sem=crecv.at[slot],
            device_id=(z, peer(0)),
            device_id_type=MESH,
        )

    where = {}
    for stage in range(1, stages):
        for stream in range(2):
            for slot, m in enumerate(held(orders[stream], stage, cols_n)):
                where[stage, stream, m] = (slot, len(where))

    def hop(stage, stream, m):
        bit = orders[stream][stage]
        slot, at = where[stage, stream, m]
        return pltpu.make_async_remote_copy(
            src_ref=sums.at[stream, m | (1 << bit)],
            dst_ref=recvs[stage].at[stream, slot],
            send_sem=hsend.at[at],
            recv_sem=hrecv.at[at],
            device_id=(z, peer(bit)),
            device_id_type=MESH,
        )

    def start_hop(stage, stream, m, it):
        at = where[stage, stream, m][1]

        @pl.when(it > 0)
        def _():
            pl.semaphore_wait(hfree.at[at], 1)

        hop(stage, stream, m).start()

    def sends_of(stage, stream):
        return [m for m in held(orders[stream], stage, cols_n)]

    def finish_hop(stage, stream, m, it, last):
        bit = orders[stream][stage]
        slot, at = where[stage, stream, m]
        hop(stage, stream, m).wait()
        added = sums[stream, m] + recvs[stage][stream, slot]
        if last:
            high = added.astype(jnp.bfloat16)
            rows = slice(stream * half_rows, (stream + 1) * half_rows)
            update[cyc_of(it), 0, rows] = high
            update[cyc_of(it), 1, rows] = (added - high.astype(jnp.float32)).astype(jnp.bfloat16)
        else:
            sums[stream, m] = added

        @pl.when(it < cycles - 1)
        def _():
            pl.semaphore_signal(hfree.at[at], inc=1, device_id=(z, peer(bit)), device_id_type=MESH)

        if not last:
            following = orders[stream][stage + 1]
            if m & (1 << following):
                start_hop(stage + 1, stream, m ^ (1 << following), it)

    def finish_last(it):
        for stream in range(2):
            finish_hop(stages - 1, stream, 0, it, True)
        panel_step(it)

    def chunk(it, _):
        cyc = cyc_of(it)
        arrive(cyc, False)
        factor_start(cyc)

        def split_left(source, _):
            rows = pl.ds(pl.multiple_of(source * blk, blk), blk)
            for group in range(groups):
                value = -land[cyc, source, group]
                high = value.astype(jnp.bfloat16)
                low = (value - high.astype(jnp.float32)).astype(jnp.bfloat16)
                cols = group * lanes_n
                left[rows, cols : cols + lanes_n] = high
                left[rows, depth + cols : depth + cols + lanes_n] = low
                left[rows, 2 * depth + cols : 2 * depth + cols + lanes_n] = high
            return 0

        lax.fori_loop(0, rows_n, split_left, 0)

        def share_step(k, _):
            m = m_of(k)
            s = lax.bitwise_xor(m, c)
            at = it * cols_n + k
            slot = lax.rem(at, 2)
            raw_copy(k, slot).wait()

            @pl.when(at + 1 < cycles * cols_n)
            def _():
                raw_copy(lax.rem(k + 1, cols_n), 1 - slot).start()

            for group in range(groups):
                value = raw[slot, :, group].reshape(share, lanes_n)
                high = value.astype(jnp.bfloat16)
                low = (value - high.astype(jnp.float32)).astype(jnp.bfloat16)
                cols = group * lanes_n
                right[:, cols : cols + lanes_n] = high
                right[:, depth + cols : depth + cols + lanes_n] = high
                right[:, 2 * depth + cols : 2 * depth + cols + lanes_n] = low

            @pl.when(it == 0)
            def _():
                for group in range(groups):
                    value = raw[slot, :, group].reshape(-1, 8, lanes_n)
                    squares[1] += jnp.sum(value * value, axis=0)

            @pl.when(k == half)
            def _():
                @pl.when(it > 0)
                def _():
                    finish_last(it - 1)

                @pl.when(it + 1 < cycles)
                def _():
                    relay(cyc - 1)

            @pl.when((k < half) & (it > 0))
            def _():
                core_copy(m).wait_send()

            product = lax.dot_general(
                left[...], right[...], (((1,), (1,)), ((), ())),
                preferred_element_type=jnp.float32,
            )
            sums[0, m] = product[:half_rows]
            sums[1, m] = product[half_rows:]

            turn = cyc - c // rows_n
            mine = (s < steps_of) & (lax.rem(turn + ratio * cycles, ratio) == 0)

            @pl.when(mine)
            def _():
                begin = lax.rem(c, rows_n) * blk
                stream = begin // half_rows
                rows = pl.ds(pl.multiple_of(lax.rem(begin, half_rows), blk), blk)
                mark = lax.rem(lax.rem(turn + ratio * cycles, ratio * cycles) // ratio, upper_ref.shape[0])
                sums[stream, m, rows, :] += upper_ref[mark, jnp.minimum(s, steps_of - 1)]

            @pl.when(k < half)
            def _():
                @pl.when(it > 0)
                def _():
                    pl.semaphore_wait(cfree.at[m // 2], 1)

                core_copy(m).start()

            @pl.when(k >= half)
            def _():
                core_copy(m + 1).wait_recv()
                for stream in range(2):
                    sums[stream, m] += recvs[0][stream, m // 2]

                @pl.when(it < cycles - 1)
                def _():
                    pl.semaphore_signal(
                        cfree.at[m // 2], inc=1, device_id=(z, peer(0)), device_id_type=MESH
                    )

                for stream in range(2):
                    bit = orders[stream][1]
                    for target in held(orders[stream], 1, cols_n):
                        @pl.when(m == target | (1 << bit))
                        def _():
                            start_hop(1, stream, target, it)

            return 0

        lax.fori_loop(0, cols_n, share_step, 0)
        for stage in range(1, stages - 1):
            for stream in range(2):
                order = sorted(
                    held(orders[stream], stage, cols_n),
                    key=lambda m: 0 if m & (1 << orders[stream][stage + 1]) else 1,
                )
                for m in order:
                    finish_hop(stage, stream, m, it, False)
        factor_pass(cyc)
        return 0

    lax.fori_loop(0, cycles, chunk, 0)
    finish_last(cycles - 1)
    stats[me] = squares[...]

    def report(other):
        return pltpu.make_async_remote_copy(
            src_ref=squares,
            dst_ref=stats.at[me],
            send_sem=ssem,
            recv_sem=rsem,
            device_id=(other // cols_n, lax.rem(other, cols_n)),
            device_id_type=MESH,
        )

    def tell(step, _):
        report(lax.rem(me + step, everyone)).start()
        return 0

    lax.fori_loop(1, everyone, tell, 0)
    for slot in range(half):
        core_copy(2 * slot + 1).wait_send()

    def drain(at, _):
        cyc = cyc_of(at)

        @pl.when(z < rows_n - 1)
        def _():
            for t in range(rows_n):
                @pl.when(z >= t)
                def _():
                    for kind in range(2):
                        piece(kind, cyc, z - t, z + 1, 0).wait_send()

        @pl.when(z > 0)
        def _():
            for t in range(rows_n):
                @pl.when(z + t < rows_n)
                def _():
                    for kind in range(2):
                        piece(kind, cyc, z + t, z - 1, 1).wait_send()

        for e in range(1, cols_n):
            spread(cyc, c, c, e).wait_send()
        for source in range(cols_n):
            @pl.when(jnp.logical_not((source == c) & (lax.rem(c, rows_n) == z)))
            def _():
                pltpu.make_async_remote_copy(
                    src_ref=mirror_ref.at[cyc, source],
                    dst_ref=mirror_ref.at[cyc, source],
                    send_sem=msend.at[0, 0],
                    recv_sem=mrecv.at[cyc, source],
                    device_id=(z, c),
                    device_id_type=MESH,
                ).wait_recv()

        return 0

    lax.fori_loop(0, cycles, drain, 0)
    mail_wait(0)
    every = stats.at[pl.ds(0, everyone - 1)]
    reports = pltpu.make_async_remote_copy(
        src_ref=every, dst_ref=every, send_sem=ssem, recv_sem=rsem,
        device_id=(z, c), device_id_type=MESH,
    )
    reports.wait_recv()
    reports.wait_send()
    total_ref[...] = jnp.sum(stats[...], axis=0)


def mirrored_panel(
    matrix, inverse_rest, lower_below, upper_block, lower_inverse, row_devices, col_devices
):
    row_cycles, blk, groups, lanes_n = inverse_rest.shape
    cycles = lower_below.shape[0]
    depth = groups * lanes_n
    share = row_cycles * blk // col_devices
    blocks = max(share // blk, col_devices // row_devices)
    part = share // blocks
    upper_cycles = upper_block.shape[2]
    stages = col_devices.bit_length() - 1
    steps_of = cycles * blk // share
    half_rows = row_devices * blk // 2
    upper = upper_block.reshape(cycles // blocks, blocks, blk // part, part, upper_cycles, blk)
    upper = upper.transpose(4, 0, 2, 5, 1, 3).reshape(upper_cycles, steps_of, blk, share)
    wide = lower_inverse.shape[2]
    ratio = col_devices // row_devices
    outer = blocks // ratio
    orders = halvings(col_devices)
    hops = sum(len(held(orders[0], stage, col_devices)) for stage in range(1, stages)) * 2
    rows = row_devices * blk
    scratch = [
        pltpu.VMEM((cycles, row_devices, groups, blk, lanes_n), jnp.float32),
        pltpu.VMEM((2, blocks, groups, part, lanes_n), jnp.float32),
        pltpu.VMEM((rows, 3 * depth), jnp.bfloat16),
        pltpu.VMEM((share, 3 * depth), jnp.bfloat16),
        pltpu.VMEM((2, col_devices, half_rows, share), jnp.float32),
        pltpu.VMEM((cycles, 2, rows, share), jnp.bfloat16),
        pltpu.VMEM((2, rows, rows), jnp.bfloat16),
        pltpu.VMEM((row_devices, rows // wide, wide, blk), jnp.float32),
        pltpu.VMEM((rows, share), jnp.float32),
        pltpu.VMEM((row_devices, ratio, outer, blk, part), jnp.float32),
        pltpu.VMEM((2, 8, lanes_n), jnp.float32),
        pltpu.VMEM((2,) + matrix.shape[1:], jnp.float32),
        pltpu.VMEM((row_devices * col_devices, 2, 8, lanes_n), jnp.float32),
    ]
    for stage in range(stages):
        scratch.append(pltpu.VMEM((2, col_devices >> (stage + 1), half_rows, share), jnp.float32))
    scratch += [
        pltpu.SemaphoreType.DMA,
        pltpu.SemaphoreType.DMA((2,)),
        pltpu.SemaphoreType.DMA((cycles, row_devices, 2)),
        pltpu.SemaphoreType.DMA((cycles, row_devices)),
        pltpu.SemaphoreType.DMA((col_devices // 2,)),
        pltpu.SemaphoreType.DMA((col_devices // 2,)),
        pltpu.SemaphoreType.REGULAR((col_devices // 2,)),
        pltpu.SemaphoreType.DMA((hops,)),
        pltpu.SemaphoreType.DMA((hops,)),
        pltpu.SemaphoreType.REGULAR((hops,)),
        pltpu.SemaphoreType.DMA,
        pltpu.SemaphoreType.DMA((cycles, row_devices, 2)),
        pltpu.SemaphoreType.DMA((cycles, row_devices)),
        pltpu.SemaphoreType.DMA((cycles, col_devices)),
        pltpu.SemaphoreType.DMA((cycles, col_devices)),
        pltpu.SemaphoreType.DMA,
        pltpu.SemaphoreType.DMA((row_devices, ratio)),
        pltpu.SemaphoreType.DMA((cycles, col_devices)),
        pltpu.SemaphoreType.DMA((2,)),
        pltpu.SemaphoreType.DMA,
        pltpu.SemaphoreType.DMA,
    ]
    mirror, _, totals = pl.pallas_call(
        functools.partial(panel_kernel, row_devices, col_devices, steps_of),
        out_shape=(
            jax.ShapeDtypeStruct((cycles, col_devices, outer, blk, part), jnp.float32),
            jax.ShapeDtypeStruct((cycles, row_devices, col_devices, wide, blk), jnp.float32),
            jax.ShapeDtypeStruct((2, 8, lanes_n), jnp.float32),
        ),
        in_specs=[
            pl.BlockSpec(memory_space=pltpu.HBM),
            pl.BlockSpec(memory_space=pltpu.HBM),
            pl.BlockSpec(memory_space=pltpu.HBM),
            pl.BlockSpec(memory_space=pltpu.VMEM),
            pl.BlockSpec(memory_space=pltpu.VMEM),
        ],
        out_specs=(
            pl.BlockSpec(memory_space=pltpu.HBM),
            pl.BlockSpec(memory_space=pltpu.HBM),
            pl.BlockSpec(memory_space=pltpu.VMEM),
        ),
        scratch_shapes=scratch,
        compiler_params=pltpu.CompilerParams(
            collective_id=0, has_side_effects=True, vmem_limit_bytes=66_000_000
        ),
        cost_estimate=pl.CostEstimate(
            flops=6 * cycles * rows * share * col_devices * depth,
            bytes_accessed=4 * cycles * col_devices * share * depth,
            transcendentals=0,
        ),
    )(
        matrix,
        inverse_rest.transpose(0, 2, 1, 3),
        lower_below.transpose(0, 2, 1, 3),
        upper,
        lower_inverse.transpose(0, 2, 1),
    )
    return mirror, totals


def per_device(matrix, inverse_rest, upper_block, lower_below, lower_inverse):
    row_devices = lax.axis_size("row")
    col_devices = lax.axis_size("col")
    row_cycles, blk_size, col_cycles, _ = matrix.shape
    panel_cycles = lower_inverse.shape[0]
    mirror, totals = mirrored_panel(
        matrix, inverse_rest, lower_below, upper_block, lower_inverse, row_devices, col_devices
    )
    inverse_block = mirror.transpose(0, 3, 1, 2, 4).reshape(
        panel_cycles, blk_size, col_cycles, blk_size
    )
    matrix_total, inverse_total = jnp.sum(totals[0]), jnp.sum(totals[1])
    balance = jnp.sqrt(jnp.sqrt(inverse_total / matrix_total))
    return 0.5 * (balance * matrix[:panel_cycles] + inverse_block / balance)


def solution(mesh):
    in_specs = (
        P(None, "row", None, "col"),
        P(None, "row", None, "col"),
        P(None, "row", None, "col"),
        P(None, "row", None, "col"),
        P(None, "row", "col"),
    )
    out_specs = P(None, "row", None, "col")
    return jax.shard_map(
        per_device, mesh=mesh, in_specs=in_specs, out_specs=out_specs, check_vma=False
    )
```

profile of v0, /device:TPU:0, one launch (start us, length us, event | category | flops | bytes accessed | tf_op | source)
XLA Modules:
  0.0 485.1 jit_solution(14987839810046535907)
XLA Ops:
  0.0 2.0 copy.9.upper_ref
  2.0 2.0 copy.7
  4.1 468.7 %shard_map.55 = (f32[4,8,2,128,128]{4,3,2,1,0:T(8,128)}, f32[4,4,8,256,128]{4,3,2,1,0:T(8,128)}, f32[2,8,128]{2,1,0:T(8,128)}) custom-call(f32[32,128,16,128]{3,2,1,0:T(8,128)} %matrix_ref.1, f32[32,14,128,128]{3,2,1,0:T(8,128)} %bitcast.14, f32[4,14,128,128]{3,2,1,0:T(8,128)} %bitcast.15, f32[2,1,128,512]{3,2,1,0:T(8,128)} %copy.9.upper_ref, ...), custom_call_target="tpu_custom_call" | custom-call | flops 90194313216 | bytes 117440512 | tf_op jit(solution)/shard_map/pallas_call | solution.py:591
  472.8 1.3 slice_reduce_fusion
  475.5 2.5 broadcast_divide_fusion
  478.0 7.1 %fusion = f32[4,128,16,128]{3,2,1,0:T(8,128)} fusion(f32[4,128,16,128]{3,1,2,0:T(8,128)S(1)} %bitcast.11, f32[32,128,16,128]{3,2,1,0:T(8,128)} %matrix_ref.1, f32[]{:T(128)S(6)} %sqrt.7), kind=kLoop, calls=%fused_computation.1 | loop fusion | flops 3145728 | bytes 12582916 | tf_op jit(solution)/shard_map/mul | solution.py:642
where the time goes:
time: 487 us; the launch traced here: 485 us
  Pallas kernels  469 us (96%)
  other arithmetic  10.9 us (2%)
    pallas_call x1, Pallas kernels, mirrored_panel(): pl.pallas_call(functools.partial(panel_kernel, row_devices, col_devices,...  469 us

commit v1 on v0

--- a/solution.py
+++ b/solution.py
@@ -8,6 +8,9 @@
 from jax.sharding import PartitionSpec as P
 
 MESH = pl.DeviceIdType.MESH
+CUTS = 2
+AHEAD = 1
+PANES = 4
 
 
 def halvings(col_devices):
@@ -33,12 +36,15 @@
     span = tile.shape[1]
     outer = mirror_ref.shape[2]
     ratio = cols_n // rows_n
-    cycles, _, groups, blk, lanes_n = land.shape
+    units, _, groups, slim, lanes_n = land.shape
+    cycles, blk = mirror_ref.shape[0], mirror_ref.shape[3]
+    cuts = units // cycles
     depth = groups * lanes_n
     share = right.shape[0]
     half_rows = sums.shape[2]
     blocks, part = raw.shape[1], raw.shape[3]
     half = cols_n // 2
+    ahead = min(AHEAD, units)
     orders = halvings(cols_n)
     z, c = lax.axis_index("row"), lax.axis_index("col")
 
@@ -46,7 +52,7 @@
         return lax.bitwise_xor(c, jnp.int32(1 << bit))
 
     def cyc_of(it):
-        return cycles - 1 - it
+        return cycles - 1 - it // cuts
 
     barrier = pltpu.get_barrier_semaphore()
     me = z * cols_n + c
@@ -60,8 +66,13 @@
         return 0
 
     lax.fori_loop(1, everyone, greet, 0)
-    own = pltpu.make_async_copy(below_ref, land.at[:, z], own_sem)
-    own.start()
+    own = []
+    for at in range(units):
+        own.append(pltpu.make_async_copy(
+            below_ref.at[cycles - 1 - at // cuts, :, pl.ds(at % cuts * slim, slim)],
+            land.at[at, z], own_sem.at[at],
+        ))
+        own[at].start()
     lower = pltpu.make_async_copy(lower_ref, factor_ref.at[:, z, c], lower_sem)
     lower.start()
 
@@ -77,85 +88,86 @@
         )
 
     raw_copy(0, 0).start()
-    own.wait()
+    for at in range(units):
+        own[at].wait()
     lower.wait()
     pl.semaphore_wait(barrier, everyone - 1)
 
-    def piece(kind, cyc, source, to, way):
-        block = factor_ref.at[cyc, source, c] if kind else land.at[cyc, source]
+    def piece(at, source, to, way):
         return pltpu.make_async_remote_copy(
-            src_ref=block,
-            dst_ref=block,
-            send_sem=(fzsend if kind else zsend).at[cyc, source, way],
-            recv_sem=(fzrecv if kind else zrecv).at[cyc, source],
+            src_ref=land.at[at, source],
+            dst_ref=land.at[at, source],
+            send_sem=zsend.at[at, source, way],
+            recv_sem=zrecv.at[at, source],
             device_id=(to, c),
             device_id_type=MESH,
         )
 
-    def send_own(cyc):
-        for kind in range(2):
-            @pl.when(z < rows_n - 1)
-            def _():
-                piece(kind, cyc, z, z + 1, 0).start()
-
-            @pl.when(z > 0)
-            def _():
-                piece(kind, cyc, z, z - 1, 1).start()
+    def factor_piece(_, source, to, way):
+        return pltpu.make_async_remote_copy(
+            src_ref=factor_ref.at[:, source, c],
+            dst_ref=factor_ref.at[:, source, c],
+            send_sem=fzsend.at[source, way],
+            recv_sem=fzrecv.at[source],
+            device_id=(to, c),
+            device_id_type=MESH,
+        )
+
+    def send_own(at, piece=piece):
+        @pl.when(z < rows_n - 1)
+        def _():
+            piece(at, z, z + 1, 0).start()
+
+        @pl.when(z > 0)
+        def _():
+            piece(at, z, z - 1, 1).start()
 
     inner = (z > 0) & (z < rows_n - 1)
 
-    def arrive(cyc, forward):
+    def arrive(at, forward, piece=piece):
         for t in range(1, rows_n):
-            for kind in range(2):
-                @pl.when((z >= t) & (inner == forward))
-                def _():
-                    piece(kind, cyc, z - t, z, 0).wait_recv()
-                    if forward:
-                        piece(kind, cyc, z - t, z + 1, 0).start()
-
-                @pl.when((z + t < rows_n) & (inner == forward))
-                def _():
-                    piece(kind, cyc, z + t, z, 0).wait_recv()
-                    if forward:
-                        piece(kind, cyc, z + t, z - 1, 1).start()
-
-    def relay(cyc):
-        arrive(cyc, True)
-
-        @pl.when(inner & (cyc > 0))
-        def _():
-            send_own(cyc - 1)
-
-    @pl.when(inner)
-    def _():
-        send_own(cycles - 1)
-
-    @pl.when(jnp.logical_not(inner))
-    def _():
-        for at in range(cycles):
-            send_own(cycles - 1 - at)
-
-    relay(cycles - 1)
-
-    def pane_copy(at, slot):
-        return pltpu.make_async_copy(matrix_ref.at[at], panes.at[slot], pane_sem.at[slot])
-
-    pane_copy(0, 0).start()
-    squares[...] = jnp.zeros_like(squares)
-
-    def pane_step(at, _):
-        slot = lax.rem(at, 2)
-        pane_copy(at, slot).wait()
-
-        @pl.when(at + 1 < matrix_ref.shape[0])
-        def _():
-            pane_copy(at + 1, 1 - slot).start()
-
-        value = panes[slot].reshape(-1, 8, lanes_n)
-        squares[0] += jnp.sum(value * value, axis=0)
-        return 0
-
-    lax.fori_loop(0, matrix_ref.shape[0], pane_step, 0)
+            @pl.when((z >= t) & (inner == forward))
+            def _():
+                piece(at, z - t, z, 0).wait_recv()
+                if forward:
+                    piece(at, z - t, z + 1, 0).start()
+
+            @pl.when((z + t < rows_n) & (inner == forward))
+            def _():
+                piece(at, z + t, z, 0).wait_recv()
+                if forward:
+                    piece(at, z + t, z - 1, 1).start()
+
+    def lead(t):
+        return ahead + rows_n - 2 - t
+
+    def relay(at, t):
+        @pl.when(inner & (z >= t))
+        def _():
+            piece(at, z - t, z, 0).wait_recv()
+            piece(at, z - t, z + 1, 0).start()
+
+        @pl.when(inner & (z + t < rows_n))
+        def _():
+            piece(at, z + t, z, 0).wait_recv()
+            piece(at, z + t, z - 1, 1).start()
+
+        if t == 1:
+            @pl.when(inner & (at + 1 < units))
+            def _():
+                send_own(at + 1)
+
+    def relay_first(begin, end):
+        for at in range(begin, min(end, units)):
+            for t in range(1, rows_n - 1):
+                if at < lead(t):
+                    relay(at, t)
+
+    def relay_later(it):
+        for t in range(rows_n - 2, 0, -1):
+            @pl.when(it + lead(t) < units)
+            def _():
+                relay(it + lead(t), t)
 
     def spread(cyc, source, to, at):
         return pltpu.make_async_remote_copy(
@@ -167,26 +179,102 @@
             device_id_type=MESH,
         )
 
+    def used(cyc, source):
+        return source * wide < (cyc + 1) * (rows_n * blk)
+
     def factor_start(cyc):
         for e in [1] + list(range(2, cols_n, 2)):
-            spread(cyc, c, lax.bitwise_xor(c, jnp.int32(e)), e).start()
+            @pl.when(used(cyc, c))
+            def _():
+                spread(cyc, c, lax.bitwise_xor(c, jnp.int32(e)), e).start()
 
     def factor_pass(cyc):
         for e in range(2, cols_n, 2):
             other = lax.bitwise_xor(c, jnp.int32(e))
-            spread(cyc, other, other, e).wait_recv()
-            spread(cyc, other, peer(0), e ^ 1).start()
+
+            @pl.when(used(cyc, other))
+            def _():
+                spread(cyc, other, other, e).wait_recv()
+                spread(cyc, other, peer(0), e ^ 1).start()
 
     def factor_wait(cyc):
         for e in range(1, cols_n, 2):
             other = lax.bitwise_xor(c, jnp.int32(e))
-            spread(cyc, other, other, e).wait_recv()
+
+            @pl.when(used(cyc, other))
+            def _():
+                spread(cyc, other, other, e).wait_recv()
+
+    def factor_sent(cyc):
+        for e in [1] + list(range(2, cols_n, 2)):
+            @pl.when(used(cyc, c))
+            def _():
+                spread(cyc, c, c, e).wait_send()
+
+        for e in range(2, cols_n, 2):
+            @pl.when(used(cyc, lax.bitwise_xor(c, jnp.int32(e))))
+            def _():
+                spread(cyc, c, c, e ^ 1).wait_send()
+
+    early = range(cycles - 1, max(cycles - 3, -1), -1)
+
+    send_own(0, factor_piece)
+
+    @pl.when(inner)
+    def _():
+        send_own(0)
+
+    @pl.when(jnp.logical_not(inner))
+    def _():
+        for at in range(units):
+            send_own(at)
+
+    arrive(0, True, factor_piece)
+
+    @pl.when(inner)
+    def _():
+        for at in early:
+            factor_start(at)
+
+    relay_first(0, 1)
+
+    def pane_copy(at, slot):
+        return pltpu.make_async_copy(matrix_ref.at[at], panes.at[slot], pane_sem.at[slot])
+
+    depth_of = panes.shape[0]
+    for at in range(depth_of - 1):
+        pane_copy(at, at).start()
+    squares[...] = jnp.zeros_like(squares)
+
+    def pane_step(at, _):
+        slot = lax.rem(at, depth_of)
+        later = at + depth_of - 1
+        pane_copy(at, slot).wait()
+
+        @pl.when(later < matrix_ref.shape[0])
+        def _():
+            pane_copy(later, lax.rem(later, depth_of)).start()
+
+        value = panes[slot].reshape(-1, 8, lanes_n)
+        squares[0] += jnp.sum(value * value, axis=0)
+        return 0
+
+    lax.fori_loop(0, matrix_ref.shape[0], pane_step, 0)
+
+    arrive(0, False, factor_piece)
+
+    @pl.when(jnp.logical_not(inner))
+    def _():
+        for at in early:
+            factor_start(at)
+
+    relay_first(1, lead(1))
 
     def away(cyc, to, turn):
         return pltpu.make_async_remote_copy(
-            src_ref=outbox.at[to, turn],
+            src_ref=outbox.at[cyc, to, turn],
             dst_ref=mirror_ref.at[cyc, c],
-            send_sem=msend.at[to, turn],
+            send_sem=msend.at[cyc, to, turn],
             recv_sem=mrecv.at[cyc, c],
             device_id=(to, turn * rows_n + z),
             device_id_type=MESH,
@@ -194,7 +282,7 @@
 
     def at_home(cyc, to, turn):
         return pltpu.make_async_copy(
-            outbox.at[to, turn], mirror_ref.at[cyc, c], msend.at[to, turn]
+            outbox.at[cyc, to, turn], mirror_ref.at[cyc, c], msend.at[cyc, to, turn]
         )
 
     def is_home(to, turn):
@@ -211,10 +299,7 @@
                 def _():
                     away(cyc, to, turn).wait_send()
 
-    def panel_step(it):
-        cyc = cyc_of(it)
-        factor_wait(cyc)
-
+    def tiles(cyc, first, last):
         def tile_step(back, _):
             from_cyc = cycles - 1 - back
             copy = pltpu.make_async_copy(
@@ -246,11 +331,9 @@
 
             return 0
 
-        lax.fori_loop(0, it + 1, tile_step, 0)
-
-        @pl.when(it > 0)
-        def _():
-            mail_wait(cyc + 1)
+        lax.fori_loop(first, last, tile_step, 0)
+
+    def fill(cyc):
 
         for to in range(rows_n):
             value = total[to * blk : (to + 1) * blk, :]
@@ -261,7 +344,9 @@
             for turn in range(ratio):
                 for place in range(outer):
                     begin = (place * ratio + turn) * part
-                    outbox[to, turn, place] = value[:, begin : begin + part]
+                    outbox[cyc, to, turn, place] = value[:, begin : begin + part]
+
+    def mail(cyc):
         for to in range(rows_n):
             for turn in range(ratio):
                 @pl.when(is_home(to, turn))
@@ -320,13 +405,17 @@
         added = sums[stream, m] + recvs[stage][stream, slot]
         if last:
             high = added.astype(jnp.bfloat16)
-            rows = slice(stream * half_rows, (stream + 1) * half_rows)
-            update[cyc_of(it), 0, rows] = high
-            update[cyc_of(it), 1, rows] = (added - high.astype(jnp.float32)).astype(jnp.bfloat16)
+            low = (added - high.astype(jnp.float32)).astype(jnp.bfloat16)
+            for place in range(half_rows // slim):
+                source = stream * (half_rows // slim) + place
+                begin = pl.multiple_of(source * blk + lax.rem(it, cuts) * slim, slim)
+                part_rows = slice(place * slim, (place + 1) * slim)
+                update[cyc_of(it), 0, pl.ds(begin, slim)] = high[part_rows]
+                update[cyc_of(it), 1, pl.ds(begin, slim)] = low[part_rows]
         else:
             sums[stream, m] = added
 
-        @pl.when(it < cycles - 1)
+        @pl.when(it < units - 1)
         def _():
             pl.semaphore_signal(hfree.at[at], inc=1, device_id=(z, peer(bit)), device_id_type=MESH)
 
@@ -338,17 +427,40 @@
     def finish_last(it):
         for stream in range(2):
             finish_hop(stages - 1, stream, 0, it, True)
-        panel_step(it)
+
+        @pl.when(lax.rem(it, cuts) == cuts - 1)
+        def _():
+            factor_wait(cyc_of(it))
+            tiles(cyc_of(it), 0, cycles - cyc_of(it))
+            fill(cyc_of(it))
+
+    def finish_mid(it):
+        for stage in range(1, stages - 1):
+            for stream in range(2):
+                order = sorted(
+                    held(orders[stream], stage, cols_n),
+                    key=lambda m: 0 if m & (1 << orders[stream][stage + 1]) else 1,
+                )
+                for m in order:
+                    finish_hop(stage, stream, m, it, False)
 
     def chunk(it, _):
         cyc = cyc_of(it)
-        arrive(cyc, False)
-        factor_start(cyc)
+        arrive(it, False)
+
+        @pl.when(it == units - 1)
+        def _():
+            for at in range(cycles - 1, 0, -1):
+                mail(at)
+
+        @pl.when((it >= cuts) & (lax.rem(it, cuts) == 0) & (cyc > 0))
+        def _():
+            factor_start(cyc - 1)
 
         def split_left(source, _):
-            rows = pl.ds(pl.multiple_of(source * blk, blk), blk)
+            rows = pl.ds(pl.multiple_of(source * slim, slim), slim)
             for group in range(groups):
-                value = -land[cyc, source, group]
+                value = -land[it, source, group]
                 high = value.astype(jnp.bfloat16)
                 low = (value - high.astype(jnp.float32)).astype(jnp.bfloat16)
                 cols = group * lanes_n
@@ -366,7 +478,7 @@
             slot = lax.rem(at, 2)
             raw_copy(k, slot).wait()
 
-            @pl.when(at + 1 < cycles * cols_n)
+            @pl.when(at + 1 < units * cols_n)
             def _():
                 raw_copy(lax.rem(k + 1, cols_n), 1 - slot).start()
 
@@ -391,9 +503,11 @@
                 def _():
                     finish_last(it - 1)
 
-                @pl.when(it + 1 < cycles)
-                def _():
-                    relay(cyc - 1)
+                relay_later(it)
+
+            @pl.when((k == 1) & (it > 0))
+            def _():
+                finish_mid(it - 1)
 
             @pl.when((k < half) & (it > 0))
             def _():
@@ -411,11 +525,12 @@
 
             @pl.when(mine)
             def _():
-                begin = lax.rem(c, rows_n) * blk
+                begin = lax.rem(c, rows_n) * slim
                 stream = begin // half_rows
-                rows = pl.ds(pl.multiple_of(lax.rem(begin, half_rows), blk), blk)
+                rows = pl.ds(pl.multiple_of(lax.rem(begin, half_rows), slim), slim)
+                taken = pl.ds(pl.multiple_of(lax.rem(it, cuts) * slim, slim), slim)
                 mark = lax.rem(lax.rem(turn + ratio * cycles, ratio * cycles) // ratio, upper_ref.shape[0])
-                sums[stream, m, rows, :] += upper_ref[mark, jnp.minimum(s, steps_of - 1)]
+                sums[stream, m, rows, :] += upper_ref[mark, jnp.minimum(s, steps_of - 1), taken]
 
             @pl.when(k < half)
             def _():
@@ -431,7 +546,7 @@
                 for stream in range(2):
                     sums[stream, m] += recvs[0][stream, m // 2]
 
-                @pl.when(it < cycles - 1)
+                @pl.when(it < units - 1)
                 def _():
                     pl.semaphore_signal(
                         cfree.at[m // 2], inc=1, device_id=(z, peer(0)), device_id_type=MESH
@@ -447,19 +562,26 @@
             return 0
 
         lax.fori_loop(0, cols_n, share_step, 0)
-        for stage in range(1, stages - 1):
-            for stream in range(2):
-                order = sorted(
-                    held(orders[stream], stage, cols_n),
-                    key=lambda m: 0 if m & (1 << orders[stream][stage + 1]) else 1,
-                )
-                for m in order:
-                    finish_hop(stage, stream, m, it, False)
-        factor_pass(cyc)
+
+        @pl.when(it == cuts - 1)
+        def _():
+            for at in early:
+                factor_pass(at)
+
+        @pl.when((it >= cuts) & (lax.rem(it, cuts) == cuts - 1) & (cyc > 0))
+        def _():
+            factor_pass(cyc - 1)
+
         return 0
 
-    lax.fori_loop(0, cycles, chunk, 0)
-    finish_last(cycles - 1)
+    lax.fori_loop(0, units, chunk, 0)
+    finish_mid(units - 1)
+    factor_wait(0)
+    tiles(0, 0, cycles - 1)
+    for stream in range(2):
+        finish_hop(stages - 1, stream, 0, units - 1, True)
+    tiles(0, cycles - 1, cycles)
+    fill(0)
     stats[me] = squares[...]
 
     def report(other):
@@ -477,37 +599,41 @@
         return 0
 
     lax.fori_loop(1, everyone, tell, 0)
+    mail(0)
     for slot in range(half):
         core_copy(2 * slot + 1).wait_send()
 
-    def drain(at, _):
-        cyc = cyc_of(at)
-
+    def sent(at, piece=piece):
         @pl.when(z < rows_n - 1)
         def _():
             for t in range(rows_n):
                 @pl.when(z >= t)
                 def _():
-                    for kind in range(2):
-                        piece(kind, cyc, z - t, z + 1, 0).wait_send()
+                    piece(at, z - t, z + 1, 0).wait_send()
 
         @pl.when(z > 0)
         def _():
             for t in range(rows_n):
                 @pl.when(z + t < rows_n)
                 def _():
-                    for kind in range(2):
-                        piece(kind, cyc, z + t, z - 1, 1).wait_send()
-
-        for e in range(1, cols_n):
-            spread(cyc, c, c, e).wait_send()
+                    piece(at, z + t, z - 1, 1).wait_send()
+
+    def drain(at, _):
+        sent(at)
+        return 0
+
+    lax.fori_loop(0, units, drain, 0)
+    sent(0, factor_piece)
+    def receive(cyc, _):
+        mail_wait(cyc)
+        factor_sent(cyc)
         for source in range(cols_n):
             @pl.when(jnp.logical_not((source == c) & (lax.rem(c, rows_n) == z)))
             def _():
                 pltpu.make_async_remote_copy(
                     src_ref=mirror_ref.at[cyc, source],
                     dst_ref=mirror_ref.at[cyc, source],
-                    send_sem=msend.at[0, 0],
+                    send_sem=msend.at[0, 0, 0],
                     recv_sem=mrecv.at[cyc, source],
                     device_id=(z, c),
                     device_id_type=MESH,
@@ -515,8 +641,7 @@
 
         return 0
 
-    lax.fori_loop(0, cycles, drain, 0)
-    mail_wait(0)
+    lax.fori_loop(0, cycles, receive, 0)
     every = stats.at[pl.ds(0, everyone - 1)]
     reports = pltpu.make_async_remote_copy(
         src_ref=every, dst_ref=every, send_sem=ssem, recv_sem=rsem,
@@ -539,7 +664,8 @@
     upper_cycles = upper_block.shape[2]
     stages = col_devices.bit_length() - 1
     steps_of = cycles * blk // share
-    half_rows = row_devices * blk // 2
+    cuts = CUTS
+    half_rows = row_devices * blk // cuts // 2
     upper = upper_block.reshape(cycles // blocks, blocks, blk // part, part, upper_cycles, blk)
     upper = upper.transpose(4, 0, 2, 5, 1, 3).reshape(upper_cycles, steps_of, blk, share)
     wide = lower_inverse.shape[2]
@@ -549,27 +675,27 @@
     hops = sum(len(held(orders[0], stage, col_devices)) for stage in range(1, stages)) * 2
     rows = row_devices * blk
     scratch = [
-        pltpu.VMEM((cycles, row_devices, groups, blk, lanes_n), jnp.float32),
+        pltpu.VMEM((cycles * cuts, row_devices, groups, blk // cuts, lanes_n), jnp.float32),
         pltpu.VMEM((2, blocks, groups, part, lanes_n), jnp.float32),
-        pltpu.VMEM((rows, 3 * depth), jnp.bfloat16),
+        pltpu.VMEM((rows // cuts, 3 * depth), jnp.bfloat16),
         pltpu.VMEM((share, 3 * depth), jnp.bfloat16),
         pltpu.VMEM((2, col_devices, half_rows, share), jnp.float32),
         pltpu.VMEM((cycles, 2, rows, share), jnp.bfloat16),
         pltpu.VMEM((2, rows, rows), jnp.bfloat16),
         pltpu.VMEM((row_devices, rows // wide, wide, blk), jnp.float32),
         pltpu.VMEM((rows, share), jnp.float32),
-        pltpu.VMEM((row_devices, ratio, outer, blk, part), jnp.float32),
+        pltpu.VMEM((cycles, row_devices, ratio, outer, blk, part), jnp.float32),
         pltpu.VMEM((2, 8, lanes_n), jnp.float32),
-        pltpu.VMEM((2,) + matrix.shape[1:], jnp.float32),
+        pltpu.VMEM((PANES,) + matrix.shape[1:], jnp.float32),
         pltpu.VMEM((row_devices * col_devices, 2, 8, lanes_n), jnp.float32),
     ]
     for stage in range(stages):
         scratch.append(pltpu.VMEM((2, col_devices >> (stage + 1), half_rows, share), jnp.float32))
     scratch += [
-        pltpu.SemaphoreType.DMA,
+        pltpu.SemaphoreType.DMA((cycles * cuts,)),
         pltpu.SemaphoreType.DMA((2,)),
-        pltpu.SemaphoreType.DMA((cycles, row_devices, 2)),
-        pltpu.SemaphoreType.DMA((cycles, row_devices)),
+        pltpu.SemaphoreType.DMA((cycles * cuts, row_devices, 2)),
+        pltpu.SemaphoreType.DMA((cycles * cuts, row_devices)),
         pltpu.SemaphoreType.DMA((col_devices // 2,)),
         pltpu.SemaphoreType.DMA((col_devices // 2,)),
         pltpu.SemaphoreType.REGULAR((col_devices // 2,)),
@@ -577,14 +703,14 @@
         pltpu.SemaphoreType.DMA((hops,)),
         pltpu.SemaphoreType.REGULAR((hops,)),
         pltpu.SemaphoreType.DMA,
-        pltpu.SemaphoreType.DMA((cycles, row_devices, 2)),
-        pltpu.SemaphoreType.DMA((cycles, row_devices)),
+        pltpu.SemaphoreType.DMA((row_devices, 2)),
+        pltpu.SemaphoreType.DMA((row_devices,)),
         pltpu.SemaphoreType.DMA((cycles, col_devices)),
         pltpu.SemaphoreType.DMA((cycles, col_devices)),
         pltpu.SemaphoreType.DMA,
-        pltpu.SemaphoreType.DMA((row_devices, ratio)),
+        pltpu.SemaphoreType.DMA((cycles, row_devices, ratio)),
         pltpu.SemaphoreType.DMA((cycles, col_devices)),
-        pltpu.SemaphoreType.DMA((2,)),
+        pltpu.SemaphoreType.DMA((PANES,)),
         pltpu.SemaphoreType.DMA,
         pltpu.SemaphoreType.DMA,
     ]

time: 487 us -> 415 us (0.85)
  Pallas kernels: 469 us -> 394 us
    pallas_call x1, Pallas kernels: 469 us -> 394 us  [mirrored_panel(): pl.pallas_call(functools.partial(panel_kernel, row_devices, col_devices,...]
where the time goes in v1:
time: 415 us; the launch traced here: 411 us
  Pallas kernels  394 us (95%)
  other arithmetic  10.9 us (3%)
    pallas_call x1, Pallas kernels, mirrored_panel(): pl.pallas_call(functools.partial(panel_kernel, row_devices, col_devices,...  394 us

profile of v1, /device:TPU:0, one launch (start us, length us, event | category | flops | bytes accessed | tf_op | source)
XLA Modules:
  0.0 410.5 jit_solution(7958751548801325252)
XLA Ops:
  0.0 2.0 copy.9.upper_ref
  2.0 2.0 copy.7
  4.1 394.1 %shard_map.55 = (f32[4,8,2,128,128]{4,3,2,1,0:T(8,128)}, f32[4,4,8,256,128]{4,3,2,1,0:T(8,128)}, f32[2,8,128]{2,1,0:T(8,128)}) custom-call(f32[32,128,16,128]{3,2,1,0:T(8,128)} %matrix_ref.1, f32[32,14,128,128]{3,2,1,0:T(8,128)} %bitcast.14, f32[4,14,128,128]{3,2,1,0:T(8,128)} %bitcast.15, f32[2,1,128,512]{3,2,1,0:T(8,128)} %copy.9.upper_ref, ...), custom_call_target="tpu_custom_call" | custom-call | flops 90194313216 | bytes 117440512 | tf_op jit(solution)/shard_map/pallas_call | solution.py:717
  398.2 1.3 slice_reduce_fusion
  400.9 2.5 broadcast_divide_fusion
  403.4 7.1 %fusion = f32[4,128,16,128]{3,2,1,0:T(8,128)} fusion(f32[4,128,16,128]{3,1,2,0:T(8,128)S(1)} %bitcast.11, f32[32,128,16,128]{3,2,1,0:T(8,128)} %matrix_ref.1, f32[]{:T(128)S(6)} %sqrt.7), kind=kLoop, calls=%fused_computation.1 | loop fusion | flops 3145728 | bytes 12582916 | tf_op jit(solution)/shard_map/mul | solution.py:768
